TPU v7x, 32 devices: a whole 2x2x4 slice. The times are simulated.
32 devices in a mesh: gx: 8 (over y, x, core), gy: 4 (over z).
Axes of the slice: x: 2, y: 2, z: 4, core: 2. Of those that a mesh axis runs over, the one named last changes fastest.
Arguments:
- field: float32 [65536, 512], P(('gx', 'gy')), may hold values from -6 to 6
Outputs:
- spectrum: float32 [65536, 512], P('gx', 'gy')
All inputs are finite; a program needn't handle non-finite values.
Results may differ from a plain program's by a relative error of at most 0.00007.
Values sent between devices are 32-bit elements; how exact they have to be, the bound alone decides.
A program may use at most 64 MiB of HBM per device.

v0:
```python
import math
import jax
import jax.numpy as jnp
from jax import lax
from jax.sharding import PartitionSpec as P

P_SIZE = 256
Q = 256
highest = lax.Precision.HIGHEST


def mat_dot(left, right):
    return jnp.dot(left, right, precision=highest, preferred_element_type=jnp.float32)


def finish(spec_real, spec_imag, frequency):
    length = P_SIZE * Q
    phases = math.pi / (2.0 * length) * frequency.astype(jnp.float32)
    factor = math.sqrt(2.0 / length)
    return factor * (
        jnp.cos(phases)[:, :, None] * spec_real + jnp.sin(phases)[:, :, None] * spec_imag
    )


def body(field):
    groups = lax.axis_size("gx")
    position = lax.axis_index("gx")
    length = P_SIZE * Q
    joined = lax.all_to_all(field, "gy", split_axis=1, concat_axis=0, tiled=True)
    row_count = joined.shape[0]
    col_width = joined.shape[1]
    half_rows = P_SIZE // (2 * groups)
    local_q = Q // groups
    local_p = P_SIZE // groups
    paired = joined.reshape(row_count // 2, 2, col_width)
    even_rows = paired[:, 0].reshape(half_rows, Q, col_width)
    odd_rows = jnp.flip(paired[:, 1].reshape(half_rows, Q, col_width), axis=1)
    low_half, high_half = (
        lax.all_to_all(even_rows, "gx", split_axis=1, concat_axis=0, tiled=True),
        lax.all_to_all(odd_rows, "gx", split_axis=1, concat_axis=0, tiled=True),
    )
    freq_first = jnp.arange(P_SIZE, dtype=jnp.int32)
    place_low = jnp.arange(P_SIZE // 2, dtype=jnp.int32)
    place_high = P_SIZE - 1 - place_low
    two_pi = 2.0 * math.pi
    low_phase = (
        two_pi / P_SIZE * (freq_first[:, None] * place_low[None, :] % P_SIZE).astype(jnp.float32)
    )
    high_phase = (
        two_pi / P_SIZE * (freq_first[:, None] * place_high[None, :] % P_SIZE).astype(jnp.float32)
    )
    flat_low = low_half.reshape(P_SIZE // 2, local_q * col_width)
    flat_high = high_half.reshape(P_SIZE // 2, local_q * col_width)
    cos_part = (
        mat_dot(jnp.cos(low_phase), flat_low) + mat_dot(jnp.cos(high_phase), flat_high)
    ).reshape(P_SIZE, local_q, col_width)
    sin_part = (
        mat_dot(jnp.sin(low_phase), flat_low) + mat_dot(jnp.sin(high_phase), flat_high)
    ).reshape(P_SIZE, local_q, col_width)
    part_imag = -sin_part
    second_place = position * local_q + jnp.arange(local_q, dtype=jnp.int32)
    turn_phase = (
        two_pi / length * (freq_first[:, None] * second_place[None, :] % length).astype(jnp.float32)
    )
    turn_cos = jnp.cos(turn_phase)[:, :, None]
    turn_sin = jnp.sin(turn_phase)[:, :, None]
    turned_real = cos_part * turn_cos + part_imag * turn_sin
    turned_imag = part_imag * turn_cos - cos_part * turn_sin
    moved_real, moved_imag = (
        lax.all_to_all(turned_real, "gx", split_axis=0, concat_axis=1, tiled=True),
        lax.all_to_all(turned_imag, "gx", split_axis=0, concat_axis=1, tiled=True),
    )
    second_index = jnp.arange(Q, dtype=jnp.int32)
    row_phase = two_pi / Q * (second_index[:, None] * second_index[None, :] % Q).astype(jnp.float32)
    row_cos = jnp.cos(row_phase)
    row_sin = jnp.sin(row_phase)
    spec_real = jnp.einsum("jb,kbc->jkc", row_cos, moved_real, precision=highest) + jnp.einsum(
        "jb,kbc->jkc", row_sin, moved_imag, precision=highest
    )
    spec_imag = jnp.einsum("jb,kbc->jkc", row_cos, moved_imag, precision=highest) - jnp.einsum(
        "jb,kbc->jkc", row_sin, moved_real, precision=highest
    )
    block_rows = lax.dynamic_slice_in_dim(freq_first, position * local_p, local_p, 0)
    frequency = block_rows[None, :] + P_SIZE * second_index[:, None]
    result = finish(spec_real, spec_imag, frequency)
    arrived = lax.all_to_all(result, "gx", split_axis=0, concat_axis=1, tiled=True)
    return arrived.reshape(local_q * P_SIZE, col_width)


def solution(mesh):
    in_specs = (P(("gx", "gy"), None),)
    out_specs = P("gx", "gy")
    return jax.shard_map(body, mesh=mesh, in_specs=in_specs, out_specs=out_specs, check_vma=False)
```

profile of v0, /device:TPU:0, one launch (start us, length us, event | category | flops | bytes accessed | tf_op | source)
XLA Modules:
  0.0 380.9 jit_solution(13258083812697321297)
XLA Ops:
  0.0 5.3 %copy.15 = f32[2048,512]{0,1:T(8,128)} copy(f32[2048,512]{1,0:T(8,128)} %param.1) | data formatting | bytes 8388608 | tf_op args[0]
  5.3 100.6 %all_to_all.97 = f32[2048,4,128]{0,2,1:T(8,128)} all-to-all(f32[2048,4,128]{0,2,1:T(8,128)} %bitcast.81), channel_id=1, replica_groups=mesh['gx'=8,'gy'=4] {'gy'}, dimensions={1} | all-to-all | bytes 8388608 | tf_op jit(solution)/shard_map/all_to_all | solution.py:29
  105.9 5.3 %copy.16 = f32[4,2048,128]{2,1,0:T(8,128)} copy(f32[4,2048,128]{1,2,0:T(8,128)} %bitcast.79) | data formatting | bytes 8388608 | tf_op jit(solution)/shard_map/all_to_all | solution.py:29
  111.2 7.7 %fusion.96 = (f32[4096,1,128]{2,1,0:T(1,128)}, f32[4096,1,128]{2,1,0:T(1,128)S(1)}) fusion(f32[4096,2,128]{2,1,0:T(2,128)} %bitcast.78), kind=kLoop, calls=%fused_computation.111 | loop fusion | bytes 8388608 | tf_op jit(solution)/shard_map/slice | solution.py:37
  118.9 2.5 copy.17
  121.4 3.8 all-to-all-start.1
  125.2 4.1 %copy.20 = f32[16,256,128]{2,0,1:T(8,128)} copy(f32[16,256,128]{2,1,0:T(8,128)} %bitcast.83) | data formatting | bytes 4194304 | tf_op jit(solution)/shard_map/reshape;squeeze | solution.py:37
  129.3 3.1 rev.4
  132.4 19.4 %all-to-all-done.1 = f32[16,256,128]{2,0,1:T(8,128)S(1)} async-done(((f32[16,256,128]{2,0,1:T(8,128)}), f32[16,256,128]{2,0,1:T(8,128)S(1)}, u32[]{:S(2)}, u32[]{:S(2)}) %all-to-all-start.1) | async-done | bytes 2097184 | tf_op jit(solution)/shard_map/all_to_all | solution.py:39
  151.8 4.9 %all-to-all-start.2 = ((f32[16,256,128]{2,0,1:T(8,128)}), f32[16,256,128]{2,0,1:T(8,128)}, u32[]{:S(2)}, u32[]{:S(2)}) async-start(f32[16,256,128]{2,0,1:T(8,128)} %rev.4), calls=%async_computation.2 | async-start | bytes 4194304 | tf_op jit(solution)/shard_map/all_to_all | solution.py:40
  156.7 0.5 fusion.57
  157.3 0.6 copy.19
  157.9 7.3 %fusion.9 = f32[256,4096]{1,0:T(8,128)} fusion(f32[16,8,32,128]{3,2,1,0:T(8,128)S(1)} %bitcast.73), kind=kOutput, calls=%fused_computation.16 | convolution fusion | flops 1611071488 | bytes 6291456 | tf_op jit(solution)/shard_map/dot_general | solution.py:13
  165.2 7.5 %fusion.7 = f32[256,4096]{1,0:T(8,128)} fusion(f32[16,8,32,128]{3,2,1,0:T(8,128)S(1)} %bitcast.74), kind=kOutput, calls=%fused_computation.14 | convolution fusion | flops 1611071488 | bytes 6291456 | tf_op jit(solution)/shard_map/dot_general | solution.py:13
  172.7 10.6 %all-to-all-done.2 = f32[16,256,128]{2,0,1:T(8,128)} async-done(((f32[16,256,128]{2,0,1:T(8,128)}), f32[16,256,128]{2,0,1:T(8,128)}, u32[]{:S(2)}, u32[]{:S(2)}) %all-to-all-start.2) | async-done | bytes 2097184 | tf_op jit(solution)/shard_map/all_to_all | solution.py:40
  183.3 0.0 copy-start.3
  183.3 2.4 copy.22
  185.7 0.4 copy-done.3
  186.1 4.9 %fusion.3 = f32[32,8,32,128]{3,1,2,0:T(8,128)S(1)} fusion(f32[256,4096]{1,0:T(8,128)S(1)} %copy-done.3, f32[16,8,32,128]{3,2,1,0:T(8,128)S(1)} %bitcast.75, s32[128]{0:T(128)S(1)} %iota_subtract_fusion), kind=kOutput, calls=%fused_computation.10 | convolution fusion | flops 1612120064 | bytes 10486272 | tf_op jit(solution)/shard_map/dot_general | solution.py:13
  191.1 0.0 copy-start.2
  191.1 0.8 copy.31
  191.9 1.4 copy-done.2
  193.3 5.0 %fusion.4 = f32[32,8,32,128]{3,1,2,0:T(8,128)S(1)} fusion(f32[256,4096]{1,0:T(8,128)S(1)} %copy-done.2, f32[16,8,32,128]{3,2,1,0:T(8,128)S(1)} %bitcast.76, s32[128]{0:T(128)S(1)} %iota_subtract_fusion), kind=kOutput, calls=%fused_computation.11 | convolution fusion | flops 1613168640 | bytes 10486272 | tf_op jit(solution)/shard_map/dot_general | solution.py:13
  198.2 1.0 copy.32
  199.2 4.6 %fusion.1 = (f32[256,32,128]{2,1,0:T(8,128)}, f32[256,32,128]{2,1,0:T(8,128)S(1)}) fusion(f32[32,8,32,128]{3,2,1,0:T(8,128)S(1)} %copy.32, f32[32,8,32,128]{3,2,1,0:T(8,128)S(1)} %copy.31, f32[256,32]{1,0:T(8,128)S(1)} %get-tuple-element.12, f32[256,32]{1,0:T(8,128)S(1)} %get-tuple-element.11), kind=kLoop, calls=%fused_computation.5 | loop fusion | flops 6291456 | bytes 16842752 | tf_op jit(solution)/shard_map/add | solution.py:67
  203.8 52.3 %all_to_all.98 = f32[256,32,128]{2,1,0:T(8,128)} all-to-all(f32[256,32,128]{2,1,0:T(8,128)S(1)} %get-tuple-element.6), channel_id=1, replica_groups=mesh['gx'=8,'gy'=4] {'gx'}, dimensions={0} | all-to-all | bytes 8388608 | tf_op jit(solution)/shard_map/all_to_all | solution.py:71
  256.1 4.6 %all-to-all-start.3 = ((f32[256,32,128]{2,1,0:T(8,128)}), f32[256,32,128]{2,1,0:T(8,128)}, u32[]{:S(2)}, u32[]{:S(2)}) async-start(f32[256,32,128]{2,1,0:T(8,128)} %get-tuple-element.5), calls=%async_computation.3 | async-start | bytes 8388608 | tf_op jit(solution)/shard_map/all_to_all | solution.py:70
  260.7 0.1 dynamic_slice.3
  260.8 0.2 fusion.63
  261.0 2.8 copy.24
  263.8 7.1 %fusion.19 = f32[256,32,128]{2,0,1:T(8,128)} fusion(f32[32,256,128]{2,1,0:T(8,128)S(1)} %bitcast.71), kind=kOutput, calls=%fused_computation.29 | convolution fusion | flops 3222142976 | bytes 8388608 | tf_op jit(solution)/shard_map/jb,kbc->jkc/dot_general | solution.py:77
  270.9 7.3 %fusion.21 = f32[256,32,128]{2,0,1:T(8,128)} fusion(f32[32,256,128]{2,1,0:T(8,128)S(1)} %bitcast.72), kind=kOutput, calls=%fused_computation.31 | convolution fusion | flops 3222142976 | bytes 8388608 | tf_op jit(solution)/shard_map/jb,kbc->jkc/dot_general | solution.py:80
  278.2 31.5 %all-to-all-done.3 = f32[256,32,128]{2,1,0:T(8,128)} async-done(((f32[256,32,128]{2,1,0:T(8,128)}), f32[256,32,128]{2,1,0:T(8,128)}, u32[]{:S(2)}, u32[]{:S(2)}) %all-to-all-start.3) | async-done | bytes 4194336 | tf_op jit(solution)/shard_map/all_to_all | solution.py:70
  309.8 2.8 copy.23
  312.6 0.0 copy-start
  312.6 0.0 copy-start.1
  312.6 4.8 %fusion.23 = f32[256,32,128]{2,0,1:T(8,128)S(1)} fusion(f32[32,256,128]{2,1,0:T(8,128)S(1)} %bitcast.69), kind=kOutput, calls=%fused_computation.33 | convolution fusion | flops 3222142976 | bytes 8388608 | tf_op jit(solution)/shard_map/jb,kbc->jkc/dot_general | solution.py:77
  317.4 0.0 copy-done
  317.4 0.0 copy-done.1
  317.4 6.1 %add_multiply_fusion = f32[256,32,128]{2,0,1:T(8,128)S(1)} fusion(f32[256,32,128]{2,0,1:T(8,128)S(1)} %copy-done.1, f32[256,32,128]{2,0,1:T(8,128)S(1)} %fusion.23, f32[256,32,128]{2,0,1:T(8,128)S(1)} %copy-done, f32[32,256,128]{2,1,0:T(8,128)S(1)} %bitcast.70, f32[256,32]{0,1:T(8,128)S(1)} %get-tuple-element.10, f32[256,32]{0,1:T(8,128)S(1)} %get-tuple-element.9), kind=kOutput, calls=%fused_computation.9 | convolution fusion | flops 3228434432 | bytes 21037056 | tf_op jit(solution)/shard_map/jb,kbc->jkc/dot_general | solution.py:80
  323.5 2.7 copy.25
  326.3 51.5 %all_to_all.99 = f32[256,32,128]{2,1,0:T(8,128)S(1)} all-to-all(f32[256,32,128]{2,1,0:T(8,128)S(1)} %copy.25), channel_id=1, replica_groups=mesh['gx'=8,'gy'=4] {'gx'}, dimensions={0} | all-to-all | bytes 8388608 | tf_op jit(solution)/shard_map/all_to_all | solution.py:86
  377.8 2.7 copy.26
  (4 shorter events, 0.0 us)
Async XLA Ops:
  121.4 30.4 %all-to-all-start.1 = ((f32[16,256,128]{2,0,1:T(8,128)}), f32[16,256,128]{2,0,1:T(8,128)S(1)}, u32[]{:S(2)}, u32[]{:S(2)}) async-start(f32[16,256,128]{2,0,1:T(8,128)} %copy.17), calls=%async_computation.1 | async-start | bytes 4194304 | tf_op jit(solution)/shard_map/all_to_all | solution.py:39
  151.8 31.5 %all-to-all-start.2 = ((f32[16,256,128]{2,0,1:T(8,128)}), f32[16,256,128]{2,0,1:T(8,128)}, u32[]{:S(2)}, u32[]{:S(2)}) async-start(f32[16,256,128]{2,0,1:T(8,128)} %rev.4), calls=%async_computation.2 | async-start | bytes 4194304 | tf_op jit(solution)/shard_map/all_to_all | solution.py:40
  183.3 2.8 copy-start.3
  191.1 2.2 copy-start.2
  256.1 53.7 %all-to-all-start.3 = ((f32[256,32,128]{2,1,0:T(8,128)}), f32[256,32,128]{2,1,0:T(8,128)}, u32[]{:S(2)}, u32[]{:S(2)}) async-start(f32[256,32,128]{2,1,0:T(8,128)} %get-tuple-element.5), calls=%async_computation.3 | async-start | bytes 8388608 | tf_op jit(solution)/shard_map/all_to_all | solution.py:70
  312.6 4.8 %copy-start = (f32[256,32,128]{2,0,1:T(8,128)S(1)}, f32[256,32,128]{2,0,1:T(8,128)}, u32[]{:S(2)}) copy-start(f32[256,32,128]{2,0,1:T(8,128)} %fusion.19) | copy-start | bytes 12582916
  312.6 4.8 %copy-start.1 = (f32[256,32,128]{2,0,1:T(8,128)S(1)}, f32[256,32,128]{2,0,1:T(8,128)}, u32[]{:S(2)}) copy-start(f32[256,32,128]{2,0,1:T(8,128)} %fusion.21) | copy-start | bytes 12582916
where the time goes:
time: 386 us; the launch traced here: 381 us
  blocking collectives  204 us (53%)
  waiting for transfers between devices  61.6 us (16%)
  matrix products  50 us (13%)
  local copies, waits for them, and re-layouts  45.8 us (12%)
  starting transfers between devices  13.2 us (3%)
  other arithmetic  5.36 us (1%)
    all_to_all x1, blocking collectives, body(): lax.all_to_all(field, 'gy', split_axis=1, concat_axis=0, tiled=True)  101 us
    all_to_all x1, blocking collectives, body(): lax.all_to_all(turned_imag, 'gx', split_axis=0, concat_axis=1, tiled=True)  52.3 us
    all_to_all x1, blocking collectives, body(): lax.all_to_all(result, 'gx', split_axis=0, concat_axis=1, tiled=True)  51.5 us
    all_to_all x1, waiting for transfers between devices, body(): lax.all_to_all(turned_real, 'gx', split_axis=0, concat_axis=1, tiled=True)  31.5 us
    dot_general x4, matrix products, mat_dot(): jnp.dot(left, right, precision=highest, preferred_element_type=jnp.float32)  24.7 us
    all_to_all x1, waiting for transfers between devices, body(): lax.all_to_all(even_rows, 'gx', split_axis=1, concat_axis=0, tiled=True)  19.4 us
    all_to_all x1, waiting for transfers between devices, body(): lax.all_to_all(odd_rows, 'gx', split_axis=1, concat_axis=0, tiled=True)  10.6 us
    unnamed x11, local copies, waits for them, and re-layouts  8.93 us
  transfers between devices with their start and end apart: 3, of which 3 were waited for; matrix products, arithmetic and copies ran while one was open for 11% of the time, Pallas kernels for 0%

commit v1 on v0

--- a/solution.py
+++ b/solution.py
@@ -7,6 +7,22 @@
 P_SIZE = 256
 Q = 256
 highest = lax.Precision.HIGHEST
+
+
+def swapped_with_each(x, axis, split, join):
+    ways, here = (lax.axis_size(axis), lax.axis_index(axis))
+    width = x.shape[split] // ways
+    shape = list(x.shape)
+    shape[split] = width
+    height = shape[join]
+    shape[join] = height * ways
+    full = jnp.zeros(shape, x.dtype)
+    for mask in range(ways):
+        part = lax.dynamic_slice_in_dim(x, (here ^ mask) * width, width, axis=split)
+        if mask:
+            part = lax.ppermute(part, axis, [(d, d ^ mask) for d in range(ways)])
+        full = lax.dynamic_update_slice_in_dim(full, part, (here ^ mask) * height, axis=join)
+    return full
 
 
 def mat_dot(left, right):
@@ -36,7 +52,7 @@
     even_rows = paired[:, 0].reshape(half_rows, Q, col_width)
     odd_rows = jnp.flip(paired[:, 1].reshape(half_rows, Q, col_width), axis=1)
     low_half, high_half = (
-        lax.all_to_all(even_rows, "gx", split_axis=1, concat_axis=0, tiled=True),
+        swapped_with_each(even_rows, "gx", 1, 0),
         lax.all_to_all(odd_rows, "gx", split_axis=1, concat_axis=0, tiled=True),
     )
     freq_first = jnp.arange(P_SIZE, dtype=jnp.int32)

time: 386 us -> 384 us (level)
  waiting for transfers between devices: 61.6 us -> 66.5 us
  matrix products: 50 us -> 45.2 us
  local copies, waits for them, and re-layouts: 45.8 us -> 41.7 us
    ppermute x0 -> x7, waiting for transfers between devices: none -> 34.9 us  [swapped_with_each(): part = lax.ppermute(part, axis, [(d, d ^ mask) for d in range(ways)])]
    all_to_all x1 -> x0, waiting for transfers between devices: 19.4 us -> none  [body(): lax.all_to_all(even_rows, 'gx', split_axis=1, concat_axis=0, tiled=True)]
    all_to_all x1, waiting for transfers between devices: 10.6 us -> 0.01 us  [body(): lax.all_to_all(odd_rows, 'gx', split_axis=1, concat_axis=0, tiled=True)]
    ppermute x0 -> x7, starting transfers between devices: none -> 6.49 us  [swapped_with_each(): part = lax.ppermute(part, axis, [(d, d ^ mask) for d in range(ways)])]
    dot_general x4, matrix products: 24.7 us -> 19.9 us  [mat_dot(): jnp.dot(left, right, precision=highest, preferred_element_type=jnp.float32)]
    unnamed x11 -> x7, local copies, waits for them, and re-layouts: 8.93 us -> 6.86 us
  transfers between devices with their start and end apart: 3 -> 9, of which waited for: 3 -> 5; matrix products, arithmetic and copies ran while one was open for 11% -> 6% of each run, Pallas kernels for 0% -> 0%
where the time goes in v1:
time: 384 us; the launch traced here: 380 us
  blocking collectives  204 us (53%)
  waiting for transfers between devices  66.5 us (17%)
  matrix products  45.2 us (12%)
  local copies, waits for them, and re-layouts  41.7 us (11%)
  starting transfers between devices  15.9 us (4%)
  other arithmetic  5.57 us (1%)
    all_to_all x1, blocking collectives, body(): lax.all_to_all(field, 'gy', split_axis=1, concat_axis=0, tiled=True)  101 us
    all_to_all x1, blocking collectives, body(): lax.all_to_all(turned_imag, 'gx', split_axis=0, concat_axis=1, tiled=True)  52.3 us
    all_to_all x1, blocking collectives, body(): lax.all_to_all(result, 'gx', split_axis=0, concat_axis=1, tiled=True)  51.5 us
    ppermute x7, waiting for transfers between devices, swapped_with_each(): part = lax.ppermute(part, axis, [(d, d ^ mask) for d in range(ways)])  34.9 us
    all_to_all x1, waiting for transfers between devices, body(): lax.all_to_all(turned_real, 'gx', split_axis=0, concat_axis=1, tiled=True)  31.5 us
    dot_general x4, matrix products, mat_dot(): jnp.dot(left, right, precision=highest, preferred_element_type=jnp.float32)  19.9 us
    slice x1, local copies, waits for them, and re-layouts, body(): even_rows = paired[:, 0].reshape(half_rows, Q, col_width)  7.69 us
  transfers between devices with their start and end apart: 9, of which 5 were waited for; matrix products, arithmetic and copies ran while one was open for 6% of the time, Pallas kernels for 0%

profile of v1, /device:TPU:0, one launch (start us, length us, event | category | flops | bytes accessed | tf_op | source)
XLA Modules:
  0.0 380.0 jit_solution(12751350019084882052)
XLA Ops:
  0.0 5.3 %copy.14 = f32[2048,512]{0,1:T(8,128)} copy(f32[2048,512]{1,0:T(8,128)} %param.1) | data formatting | bytes 8388608 | tf_op args[0]
  5.3 100.6 %all_to_all.82 = f32[2048,4,128]{0,2,1:T(8,128)} all-to-all(f32[2048,4,128]{0,2,1:T(8,128)} %bitcast.77), channel_id=1, replica_groups=mesh['gx'=8,'gy'=4] {'gy'}, dimensions={1} | all-to-all | bytes 8388608 | tf_op jit(solution)/shard_map/all_to_all | solution.py:45
  105.9 5.3 %copy.15 = f32[4,2048,128]{2,1,0:T(8,128)} copy(f32[4,2048,128]{1,2,0:T(8,128)} %bitcast.75) | data formatting | bytes 8388608 | tf_op jit(solution)/shard_map/all_to_all | solution.py:45
  111.2 7.7 %fusion.96 = (f32[4096,1,128]{2,1,0:T(1,128)}, f32[4096,1,128]{2,1,0:T(1,128)S(1)}) fusion(f32[4096,2,128]{2,1,0:T(2,128)} %bitcast.74), kind=kLoop, calls=%fused_computation.126 | loop fusion | bytes 8388608 | tf_op jit(solution)/shard_map/slice | solution.py:52
  118.9 1.2 copy.16
  120.1 1.5 rev.4
  121.6 4.9 %all-to-all-start.1 = ((f32[16,256,128]{2,0,1:T(8,128)}), f32[16,256,128]{2,0,1:T(8,128)}, u32[]{:S(2)}, u32[]{:S(2)}) async-start(f32[16,256,128]{2,0,1:T(8,128)} %rev.4), calls=%async_computation.1 | async-start | bytes 4194304 | tf_op jit(solution)/shard_map/all_to_all | solution.py:56
  126.5 0.2 broadcast_in_dim.2
  126.8 2.6 constant_dynamic-slice_fusion
  129.4 0.4 collective-permute-start
  129.7 1.6 collective-permute-start.1
  131.4 0.5 fusion.57
  131.9 0.1 collective-permute-start.2
  132.0 1.7 collective-permute-start.3
  133.7 0.1 collective-permute-start.4
  133.8 0.0 collective-permute-done
  133.8 2.6 collective-permute-start.5
  136.4 1.0 constant_dynamic-update-slice_fusion.6
  137.4 20.5 %collective-permute-done.1 = f32[16,32,128]{2,1,0:T(8,128)} collective-permute-done((f32[16,32,128]{2,1,0:T(8,128)}, f32[16,32,128]{2,1,0:T(8,128)}, u32[]{:S(2)}, u32[]{:S(2)}) %collective-permute-start.1) | collective-permute-done | bytes 262176 | tf_op jit(solution)/shard_map/ppermute | solution.py:23
  157.9 0.1 collective-permute-start.6
  157.9 1.0 constant_dynamic-update-slice_fusion.5
  158.9 3.5 collective-permute-done.2
  162.4 1.0 constant_dynamic-update-slice_fusion.4
  163.3 0.0 collective-permute-done.3
  163.4 0.0 collective-permute-done.4
  163.4 6.5 %collective-permute-done.5 = f32[16,32,128]{2,1,0:T(8,128)S(1)} collective-permute-done((f32[16,32,128]{2,1,0:T(8,128)S(1)}, f32[16,32,128]{2,1,0:T(8,128)S(1)}, u32[]{:S(2)}, u32[]{:S(2)}) %collective-permute-start.5) | collective-permute-done | bytes 262176 | tf_op jit(solution)/shard_map/ppermute | solution.py:23
  169.9 4.5 %collective-permute-done.6 = f32[16,32,128]{2,1,0:T(8,128)S(1)} collective-permute-done((f32[16,32,128]{2,1,0:T(8,128)S(1)}, f32[16,32,128]{2,1,0:T(8,128)S(1)}, u32[]{:S(2)}, u32[]{:S(2)}) %collective-permute-start.6) | collective-permute-done | bytes 262176 | tf_op jit(solution)/shard_map/ppermute | solution.py:23
  174.4 0.0 all-to-all-done.1
  174.4 2.2 copy.18
  176.7 5.0 %fusion.7 = f32[256,4096]{1,0:T(8,128)S(1)} fusion(f32[16,8,32,128]{3,2,1,0:T(8,128)S(1)} %bitcast.71, s32[128]{0:T(128)S(1)} %iota_subtract_fusion), kind=kOutput, calls=%fused_computation.14 | convolution fusion | flops 1611071488 | bytes 6291968 | tf_op jit(solution)/shard_map/dot_general | solution.py:29
  181.6 5.0 %fusion.5 = f32[256,4096]{1,0:T(8,128)S(1)} fusion(f32[16,8,32,128]{3,2,1,0:T(8,128)S(1)} %bitcast.72, s32[128]{0:T(128)S(1)} %iota_subtract_fusion), kind=kOutput, calls=%fused_computation.12 | convolution fusion | flops 1611071488 | bytes 6291968 | tf_op jit(solution)/shard_map/dot_general | solution.py:29
  186.6 4.9 %fusion.3 = f32[32,8,32,128]{3,1,2,0:T(8,128)S(1)} fusion(f32[256,4096]{1,0:T(8,128)S(1)} %fusion.7, f32[16,8,32,128]{3,2,1,0:T(8,128)S(1)} %bitcast.69), kind=kOutput, calls=%fused_computation.10 | convolution fusion | flops 1612120064 | bytes 10485760 | tf_op jit(solution)/shard_map/dot_general | solution.py:29
  191.6 0.8 copy.26
  192.3 5.0 %fusion.4 = f32[32,8,32,128]{3,1,2,0:T(8,128)S(1)} fusion(f32[256,4096]{1,0:T(8,128)S(1)} %fusion.5, f32[16,8,32,128]{3,2,1,0:T(8,128)S(1)} %bitcast.70), kind=kOutput, calls=%fused_computation.11 | convolution fusion | flops 1613168640 | bytes 10485760 | tf_op jit(solution)/shard_map/dot_general | solution.py:29
  197.3 0.8 copy.27
  198.1 4.8 %fusion.1 = (f32[256,32,128]{2,1,0:T(8,128)}, f32[256,32,128]{2,1,0:T(8,128)S(1)}) fusion(f32[32,8,32,128]{3,2,1,0:T(8,128)S(1)} %copy.27, f32[32,8,32,128]{3,2,1,0:T(8,128)S(1)} %copy.26, f32[256,32]{1,0:T(8,128)S(1)} %get-tuple-element.20, f32[256,32]{1,0:T(8,128)S(1)} %get-tuple-element.19), kind=kLoop, calls=%fused_computation.5 | loop fusion | flops 6291456 | bytes 16842752 | tf_op jit(solution)/shard_map/add | solution.py:83
  202.9 52.3 %all_to_all.83 = f32[256,32,128]{2,1,0:T(8,128)} all-to-all(f32[256,32,128]{2,1,0:T(8,128)S(1)} %get-tuple-element.6), channel_id=1, replica_groups=mesh['gx'=8,'gy'=4] {'gx'}, dimensions={0} | all-to-all | bytes 8388608 | tf_op jit(solution)/shard_map/all_to_all | solution.py:87
  255.2 4.5 %all-to-all-start.2 = ((f32[256,32,128]{2,1,0:T(8,128)}), f32[256,32,128]{2,1,0:T(8,128)}, u32[]{:S(2)}, u32[]{:S(2)}) async-start(f32[256,32,128]{2,1,0:T(8,128)} %get-tuple-element.5), calls=%async_computation.2 | async-start | bytes 8388608 | tf_op jit(solution)/shard_map/all_to_all | solution.py:86
  259.8 0.1 dynamic_slice.27
  259.8 0.2 fusion.63
  260.0 2.8 copy.20
  262.9 7.1 %fusion.19 = f32[256,32,128]{2,0,1:T(8,128)} fusion(f32[32,256,128]{2,1,0:T(8,128)S(1)} %bitcast.67), kind=kOutput, calls=%fused_computation.29 | convolution fusion | flops 3222142976 | bytes 8388608 | tf_op jit(solution)/shard_map/jb,kbc->jkc/dot_general | solution.py:93
  270.0 7.3 %fusion.21 = f32[256,32,128]{2,0,1:T(8,128)} fusion(f32[32,256,128]{2,1,0:T(8,128)S(1)} %bitcast.68), kind=kOutput, calls=%fused_computation.31 | convolution fusion | flops 3222142976 | bytes 8388608 | tf_op jit(solution)/shard_map/jb,kbc->jkc/dot_general | solution.py:96
  277.3 31.5 %all-to-all-done.2 = f32[256,32,128]{2,1,0:T(8,128)} async-done(((f32[256,32,128]{2,1,0:T(8,128)}), f32[256,32,128]{2,1,0:T(8,128)}, u32[]{:S(2)}, u32[]{:S(2)}) %all-to-all-start.2) | async-done | bytes 4194336 | tf_op jit(solution)/shard_map/all_to_all | solution.py:86
  308.8 2.8 copy.19
  311.7 0.0 copy-start
  311.7 0.0 copy-start.1
  311.7 4.8 %fusion.23 = f32[256,32,128]{2,0,1:T(8,128)S(1)} fusion(f32[32,256,128]{2,1,0:T(8,128)S(1)} %bitcast.65), kind=kOutput, calls=%fused_computation.33 | convolution fusion | flops 3222142976 | bytes 8388608 | tf_op jit(solution)/shard_map/jb,kbc->jkc/dot_general | solution.py:93
  316.4 0.0 copy-done
  316.5 0.0 copy-done.1
  316.5 6.1 %add_multiply_fusion = f32[256,32,128]{2,0,1:T(8,128)S(1)} fusion(f32[256,32,128]{2,0,1:T(8,128)S(1)} %copy-done.1, f32[256,32,128]{2,0,1:T(8,128)S(1)} %fusion.23, f32[256,32,128]{2,0,1:T(8,128)S(1)} %copy-done, f32[32,256,128]{2,1,0:T(8,128)S(1)} %bitcast.66, f32[256,32]{0,1:T(8,128)S(1)} %get-tuple-element.18, f32[256,32]{0,1:T(8,128)S(1)} %get-tuple-element.17), kind=kOutput, calls=%fused_computation.9 | convolution fusion | flops 3228434432 | bytes 21037056 | tf_op jit(solution)/shard_map/jb,kbc->jkc/dot_general | solution.py:96
  322.6 2.7 copy.21
  325.3 51.5 %all_to_all.84 = f32[256,32,128]{2,1,0:T(8,128)S(1)} all-to-all(f32[256,32,128]{2,1,0:T(8,128)S(1)} %copy.21), channel_id=1, replica_groups=mesh['gx'=8,'gy'=4] {'gx'}, dimensions={0} | all-to-all | bytes 8388608 | tf_op jit(solution)/shard_map/all_to_all | solution.py:102
  376.8 2.7 copy.22
  (8 shorter events, 0.1 us)
Async XLA Ops:
  121.6 52.8 %all-to-all-start.1 = ((f32[16,256,128]{2,0,1:T(8,128)}), f32[16,256,128]{2,0,1:T(8,128)}, u32[]{:S(2)}, u32[]{:S(2)}) async-start(f32[16,256,128]{2,0,1:T(8,128)} %rev.4), calls=%async_computation.1 | async-start | bytes 4194304 | tf_op jit(solution)/shard_map/all_to_all | solution.py:56
  129.4 4.5 %collective-permute-start = (f32[16,32,128]{2,1,0:T(8,128)}, f32[16,32,128]{2,1,0:T(8,128)}, u32[]{:S(2)}, u32[]{:S(2)}) collective-permute-start(f32[16,32,128]{2,1,0:T(8,128)} %get-tuple-element.15), channel_id=1, source_target_pairs={{0,4},{4,0},{8,12},{12,8},{16,20},{20,16},{24,28},{28,24},{1,5},{5... | collective-permute-start | bytes 786440 | tf_op jit(solution)/shard_map/ppermute | solution.py:23
  129.7 28.1 %collective-permute-start.1 = (f32[16,32,128]{2,1,0:T(8,128)}, f32[16,32,128]{2,1,0:T(8,128)}, u32[]{:S(2)}, u32[]{:S(2)}) collective-permute-start(f32[16,32,128]{2,1,0:T(8,128)} %get-tuple-element.14), channel_id=1, source_target_pairs={{0,8},{4,12},{8,0},{12,4},{16,24},{20,28},{24,16},{28,20},{1,9},{5... | collective-permute-start | bytes 786440 | tf_op jit(solution)/shard_map/ppermute | solution.py:23
  131.9 30.4 %collective-permute-start.2 = (f32[16,32,128]{2,1,0:T(8,128)}, f32[16,32,128]{2,1,0:T(8,128)}, u32[]{:S(2)}, u32[]{:S(2)}) collective-permute-start(f32[16,32,128]{2,1,0:T(8,128)} %get-tuple-element.13), channel_id=1, source_target_pairs={{0,12},{4,8},{8,4},{12,0},{16,28},{20,24},{24,20},{28,16},{1,13},{... | collective-permute-start | bytes 786440 | tf_op jit(solution)/shard_map/ppermute | solution.py:23
  132.0 31.3 %collective-permute-start.3 = (f32[16,32,128]{2,1,0:T(8,128)S(1)}, f32[16,32,128]{2,1,0:T(8,128)S(1)}, u32[]{:S(2)}, u32[]{:S(2)}) collective-permute-start(f32[16,32,128]{2,1,0:T(8,128)S(1)} %get-tuple-element.12), channel_id=1, source_target_pairs={{0,16},{4,20},{8,24},{12,28},{16,0},{20,4},{24,8},{28,12},{1,17},{... | collective-permute-start | bytes 786440 | tf_op jit(solution)/shard_map/ppermute | solution.py:23
  133.7 29.6 %collective-permute-start.4 = (f32[16,32,128]{2,1,0:T(8,128)S(1)}, f32[16,32,128]{2,1,0:T(8,128)S(1)}, u32[]{:S(2)}, u32[]{:S(2)}) collective-permute-start(f32[16,32,128]{2,1,0:T(8,128)S(1)} %get-tuple-element.11), channel_id=1, source_target_pairs={{0,20},{4,16},{8,28},{12,24},{16,4},{20,0},{24,12},{28,8},{1,21},{... | collective-permute-start | bytes 786440 | tf_op jit(solution)/shard_map/ppermute | solution.py:23
  133.8 36.1 %collective-permute-start.5 = (f32[16,32,128]{2,1,0:T(8,128)S(1)}, f32[16,32,128]{2,1,0:T(8,128)S(1)}, u32[]{:S(2)}, u32[]{:S(2)}) collective-permute-start(f32[16,32,128]{2,1,0:T(8,128)S(1)} %get-tuple-element.10), channel_id=1, source_target_pairs={{0,24},{4,28},{8,16},{12,20},{16,8},{20,12},{24,0},{28,4},{1,25},{... | collective-permute-start | bytes 786440 | tf_op jit(solution)/shard_map/ppermute | solution.py:23
  157.9 16.5 %collective-permute-start.6 = (f32[16,32,128]{2,1,0:T(8,128)S(1)}, f32[16,32,128]{2,1,0:T(8,128)S(1)}, u32[]{:S(2)}, u32[]{:S(2)}) collective-permute-start(f32[16,32,128]{2,1,0:T(8,128)S(1)} %get-tuple-element.9), channel_id=1, source_target_pairs={{0,28},{4,24},{8,20},{12,16},{16,12},{20,8},{24,4},{28,0},{1,29},{... | collective-permute-start | bytes 786440 | tf_op jit(solution)/shard_map/ppermute | solution.py:23
  255.2 53.7 %all-to-all-start.2 = ((f32[256,32,128]{2,1,0:T(8,128)}), f32[256,32,128]{2,1,0:T(8,128)}, u32[]{:S(2)}, u32[]{:S(2)}) async-start(f32[256,32,128]{2,1,0:T(8,128)} %get-tuple-element.5), calls=%async_computation.2 | async-start | bytes 8388608 | tf_op jit(solution)/shard_map/all_to_all | solution.py:86
  311.7 4.8 %copy-start = (f32[256,32,128]{2,0,1:T(8,128)S(1)}, f32[256,32,128]{2,0,1:T(8,128)}, u32[]{:S(2)}) copy-start(f32[256,32,128]{2,0,1:T(8,128)} %fusion.19) | copy-start | bytes 12582916
  311.7 4.8 %copy-start.1 = (f32[256,32,128]{2,0,1:T(8,128)S(1)}, f32[256,32,128]{2,0,1:T(8,128)}, u32[]{:S(2)}) copy-start(f32[256,32,128]{2,0,1:T(8,128)} %fusion.21) | copy-start | bytes 12582916
